TPU v7x, 32 devices: a whole 2x2x4 slice. The times are simulated.
32 devices in a mesh: gx: 16 (over z, y, core), gy: 2 (over x).
Axes of the slice: x: 2, y: 2, z: 4, core: 2. Of those that a mesh axis runs over, the one named last changes fastest.
Arguments:
- right_side: float32 [16, 2, 512, 256], P('gx', 'gy'), may hold values from -8 to 8, as said below
- coords: float32 [16, 2, 2, 512], P('gx', 'gy'), may hold values from 0 to 1
- noise: float32 [16, 2, 512], P('gx', 'gy'), may hold values from 0.25 to 1
- intersect: int32 [16, 2, 128], P('gx', 'gy'), may hold values from 0 to 4607, as said below
Outputs:
- solution: float32 [16, 2, 512, 256], P('gx', 'gy')
- residual: float32 [16, 2, 512, 256], P('gx', 'gy')
Inputs may be any that keep to these rules, and one draw needn't show every extreme that they name: `right_side`: right-hand sides of order one. `intersect`: each subdomain's list holds 128 distinct indices in increasing order; none names the subdomain itself (block number 4) or a subdomain beyond the first or last one along the second dimension.
All inputs are finite; a program needn't handle non-finite values.
Results may differ from a plain program's by a relative error of at most 0.0003.
Values sent between devices are 32-bit elements; how exact they have to be, the bound alone decides.
A program may use at most 128 MiB of HBM per device.

v0:
```python
import math
import jax
import jax.numpy as jnp
from jax import lax
from jax.sharding import PartitionSpec as P

ITERS = 3
RANGE_LEN = 0.25
ROOT_THREE = math.sqrt(3.0)
HIGH = lax.Precision.HIGHEST


def shifted(value, axis, by):
    count = lax.axis_size(axis)
    return lax.ppermute(value, axis, [(i, (i + by) % count) for i in range(count)])


def passed_along(block, axis, distance):
    devices = range(lax.axis_size(axis))
    route = [(i - distance, i) for i in devices if i - distance in devices]
    return lax.ppermute(block, axis, route)


def kernel_block(rows_pos, cols_pos):
    delta_x = rows_pos[0][:, None] - cols_pos[0][None, :]
    delta_y = rows_pos[1][:, None] - cols_pos[1][None, :]
    distance = jnp.sqrt(delta_x * delta_x + delta_y * delta_y)
    scaled = ROOT_THREE / RANGE_LEN * distance
    clipped = jnp.minimum(distance, 1.0)
    taper_val = jnp.square(jnp.square(1.0 - clipped)) * (4.0 * clipped + 1.0)
    return (1.0 + scaled) * jnp.exp(-scaled) * taper_val


def window_values(values):
    beside = {}
    for step_by in (1, -1):
        beside[step_by] = shifted(values, "gx", step_by)
    column = jnp.stack([beside[1], values, beside[-1]])
    across = {}
    for step_by in (1, -1):
        across[step_by] = passed_along(column, "gy", step_by)
    return [across[1], column, across[-1]]


def window_index(values):
    beside = {}
    for step_by in (1, -1):
        beside[step_by] = shifted(values, "gx", step_by)
    column = jnp.stack([beside[1], values, beside[-1]])
    across = {}
    for step_by in (1, -1):
        across[step_by] = passed_along(column, "gy", step_by)
    return [across[1], column, across[-1]]


def column_sum(first, second):
    return jnp.sum(first * second, axis=0)


def residual_dot(residue, precond):
    return lax.psum(column_sum(residue, precond), ("gx", "gy"))


def shards(right_side, coords, noise, intersect):
    points = right_side.shape[2]
    rhs_count = right_side.shape[3]
    intersect_len = intersect.shape[2]
    ext_len = points + intersect_len
    own_pos = coords.reshape(2, points)
    own_noise = noise.reshape(points)
    point_info = jnp.concatenate([own_pos, own_noise[None, :]], axis=0)
    info_cols = window_values(point_info)
    positions = [
        [
            jnp.stack(
                [
                    info_cols[col_off][row_off, 0] + float(row_off - 1),
                    info_cols[col_off][row_off, 1] + float(col_off - 1),
                ]
            )
            for col_off in range(3)
        ]
        for row_off in range(3)
    ]
    intersect_ids = intersect.reshape(intersect_len)
    block_id = intersect_ids // points
    row_in = intersect_ids % points
    row_of = block_id // 3
    col_of = block_id % 3
    local_id = row_of * points + row_in
    picked_info = [
        jnp.take(
            jnp.transpose(info_cols[col_off], (1, 0, 2)).reshape(3, 3 * points), local_id, axis=1
        )
        for col_off in range(3)
    ]
    chosen = jnp.where(
        col_of[None, :] == 0,
        picked_info[0],
        jnp.where(col_of[None, :] == 1, picked_info[1], picked_info[2]),
    )
    ov_pos = jnp.stack(
        [chosen[0] + (row_of - 1).astype(jnp.float32), chosen[1] + (col_of - 1).astype(jnp.float32)]
    )
    ext_pos = jnp.concatenate([own_pos, ov_pos], axis=1)
    ext_noise = jnp.concatenate([own_noise, chosen[2]])
    local_matrix = kernel_block(ext_pos, ext_pos) + jnp.diag(ext_noise)
    factor = jnp.linalg.cholesky(local_matrix)
    inv_factor = lax.linalg.triangular_solve(
        factor, jnp.eye(ext_len, dtype=jnp.float32), left_side=True, lower=True
    )
    inverse = jnp.dot(inv_factor.T, inv_factor, precision=HIGH, preferred_element_type=jnp.float32)
    near_ids = window_index(intersect_ids)
    point_iota = jnp.arange(points, dtype=jnp.int32)[:, None]
    row_base = (2 - jnp.arange(3, dtype=jnp.int32))[:, None] * 3
    selectors = []
    for col_off in range(3):
        own_rows = near_ids[col_off] - (row_base + (2 - col_off)) * points
        selectors.append((point_iota == own_rows.reshape(1, 3 * intersect_len)).astype(jnp.float32))

    def borrowed_rows(residue):
        requested = [
            lax.dot_general(
                selectors[col_off],
                residue,
                (((0,), (0,)), ((), ())),
                precision=HIGH,
                preferred_element_type=jnp.float32,
            ).reshape(3, intersect_len, rhs_count)
            for col_off in range(3)
        ]
        combined = jnp.stack([requested[col_off][1] for col_off in range(3)])
        for step_by, row_off in ((-1, 0), (1, 2)):
            outgoing = jnp.stack([requested[col_off][row_off] for col_off in range(3)])
            combined = combined + shifted(outgoing, "gx", step_by)
        gathered = combined[1]
        for step_by, col_off in ((-1, 0), (1, 2)):
            gathered = gathered + passed_along(combined[col_off], "gy", step_by)
        return gathered

    def precondition(residue):
        gathered = borrowed_rows(residue)
        extended = jnp.concatenate([residue, gathered], axis=0)
        solved = jnp.dot(inverse, extended, precision=HIGH, preferred_element_type=jnp.float32)
        returned = window_values(solved[points:])
        result = solved[:points]
        for col_off in range(3):
            result = result + jnp.dot(
                selectors[col_off],
                returned[col_off].reshape(3 * intersect_len, rhs_count),
                precision=HIGH,
                preferred_element_type=jnp.float32,
            )
        return result

    noise_col = own_noise[:, None]
    residual = right_side.reshape(points, rhs_count)
    solution = jnp.zeros_like(residual)
    precond = precondition(residual)
    direction = precond
    inner_now = residual_dot(residual, precond)
    for iteration in range(ITERS):
        columns = window_values(direction)
        accumulated = noise_col * direction
        for operate_row_off in range(3):
            for operate_col_off in range(3):
                accumulated = accumulated + jnp.dot(
                    kernel_block(own_pos, positions[operate_row_off][operate_col_off]),
                    columns[operate_col_off][operate_row_off],
                    precision=HIGH,
                    preferred_element_type=jnp.float32,
                )
        step_size = inner_now / lax.psum(column_sum(direction, accumulated), ("gx", "gy"))
        solution = solution + step_size * direction
        residual = residual - step_size * accumulated
        if iteration + 1 < ITERS:
            precond = precondition(residual)
            inner_next = residual_dot(residual, precond)
            direction = precond + inner_next / inner_now * direction
            inner_now = inner_next
    return (solution.reshape(1, 1, points, rhs_count), residual.reshape(1, 1, points, rhs_count))


def solution(mesh):
    placed = (
        P("gx", "gy", None, None),
        P("gx", "gy", None, None),
        P("gx", "gy", None),
        P("gx", "gy", None),
    )
    return jax.shard_map(
        shards,
        mesh=mesh,
        in_specs=placed,
        out_specs=(P("gx", "gy", None, None), P("gx", "gy", None, None)),
        check_vma=False,
    )
```

profile of v0, /device:TPU:0, one launch (start us, length us, event | category | flops | bytes accessed | tf_op | source)
XLA Modules:
  0.0 750.6 jit_solution(9324209336027450057)
XLA Ops:
  1.2 5.0 collective-permute-start.5
  7.0 4.4 collective-permute-start.1
  15.4 4.5 collective-permute-start.6
  23.5 3.7 collective-permute-start.2
  38.7 11.7 %cholesky.132 = f32[128,128]{1,0:T(8,128)S(1)} custom-call(f32[128,128]{1,0:T(8,128)S(1)} %cholesky.337), custom_call_target="Cholesky" | custom-call | tf_op jit(solution)/shard_map/jit(cholesky)/cholesky | solution.py:108
  50.6 9.8 %custom-call.38 = f32[1,128,128]{1,2,0:T(8,128)S(1)} custom-call(f32[1,128,128]{2,1,0:T(8,128)S(1)} %get-tuple-element.83), custom_call_target="InvertDiagBlocksLowerTriangular" | custom-call | tf_op jit(solution)/shard_map/jit(cholesky)/cholesky | solution.py:108
  63.0 11.9 %cholesky.270 = f32[128,128]{1,0:T(8,128)S(1)} custom-call(f32[128,128]{1,0:T(8,128)S(1)} %cholesky.341), custom_call_target="Cholesky" | custom-call | tf_op jit(solution)/shard_map/jit(cholesky)/cholesky | solution.py:108
  76.3 9.8 %custom-call.39 = f32[1,128,128]{1,2,0:T(8,128)S(1)} custom-call(f32[1,128,128]{2,1,0:T(8,128)S(1)} %get-tuple-element.80), custom_call_target="InvertDiagBlocksLowerTriangular" | custom-call | tf_op jit(solution)/shard_map/jit(cholesky)/cholesky | solution.py:108
  87.8 11.7 %cholesky.291 = f32[128,128]{1,0:T(8,128)S(1)} custom-call(f32[128,128]{1,0:T(8,128)S(1)} %cholesky.346), custom_call_target="Cholesky" | custom-call | tf_op jit(solution)/shard_map/jit(cholesky)/cholesky | solution.py:108
  100.3 9.8 %custom-call.40 = f32[1,128,128]{1,2,0:T(8,128)S(1)} custom-call(f32[1,128,128]{2,1,0:T(8,128)S(1)} %get-tuple-element.77), custom_call_target="InvertDiagBlocksLowerTriangular" | custom-call | tf_op jit(solution)/shard_map/jit(cholesky)/cholesky | solution.py:108
  112.0 11.7 %cholesky.310 = f32[128,128]{1,0:T(8,128)S(1)} custom-call(f32[128,128]{1,0:T(8,128)S(1)} %cholesky.351), custom_call_target="Cholesky" | custom-call | tf_op jit(solution)/shard_map/jit(cholesky)/cholesky | solution.py:108
  124.4 9.8 %custom-call.41 = f32[1,128,128]{1,2,0:T(8,128)S(1)} custom-call(f32[1,128,128]{2,1,0:T(8,128)S(1)} %get-tuple-element.74), custom_call_target="InvertDiagBlocksLowerTriangular" | custom-call | tf_op jit(solution)/shard_map/jit(cholesky)/cholesky | solution.py:108
  135.7 11.7 %cholesky.327 = f32[128,128]{1,0:T(8,128)S(1)} custom-call(f32[128,128]{1,0:T(8,128)S(1)} %convolution_subtract_fusion.6), custom_call_target="Cholesky" | custom-call | tf_op jit(solution)/shard_map/jit(cholesky)/cholesky | solution.py:108
  152.5 17.8 %while.1 = (s32[]{:T(128)}, f32[640,640]{1,0:T(8,128)}, s32[5,2]{0,1:T(2,128)S(1)}, f32[5,128,128]{2,1,0:T(8,128)}, s32[]{:T(128)}) while((s32[]{:T(128)}, f32[640,640]{1,0:T(8,128)}, s32[5,2]{0,1:T(2,128)S(1)}, f32[5,128,128]{2,1,0:T(8,128)}, s32[]{:T(128)}) %tuple.96), condition=%wide.while_cond, body=%wide.while_body.sunk | while | flops 2 | bytes 132705 | solution.py:109
  170.3 50.7 %custom-call.42 = f32[5,128,128]{1,2,0:T(8,128)} custom-call(f32[5,128,128]{2,1,0:T(8,128)} %get-tuple-element.10), custom_call_target="InvertDiagBlocksLowerTriangular" | custom-call | tf_op jit(solution)/shard_map/triangular_solve | solution.py:109
  234.1 4.7 collective-permute-start.11
  238.8 5.0 fusion.240
  245.7 4.4 collective-permute-start.13
  260.4 3.8 collective-permute-done.15
  264.9 4.4 collective-permute-start.17
  269.3 6.9 collective-permute-done.16
  285.3 26.6 %collective-permute-done.18 = f32[3,512,256]{2,1,0:T(8,128)S(1)} collective-permute-done((f32[3,512,256]{2,1,0:T(8,128)S(1)}, f32[3,512,256]{2,1,0:T(8,128)S(1)}, u32[]{:S(2)}, u32[]{:S(2)}) %collective-permute-start.18) | collective-permute-done | bytes 1572896 | tf_op jit(solution)/shard_map/ppermute | solution.py:21
  324.3 40.9 %all-reduce.1 = (f32[256]{0:T(256)S(1)}, f32[256]{0:T(256)S(1)}) all-reduce(f32[256]{0:T(256)S(1)} %get-tuple-element.12, f32[256]{0:T(256)S(1)} %get-tuple-element.11), channel_id=1, replica_groups=mesh['gx'=16,'gy'=2] {'gx','gy'}, use_global_device_ids=true, to_apply=%region_11.13 | all-reduce | flops 512 | bytes 4096 | tf_op jit(solution)/shard_map/psum | solution.py:61
  369.6 5.2 collective-permute-done.20
  374.7 4.8 collective-permute-done.21
  380.9 4.6 collective-permute-start.23
  391.3 4.1 collective-permute-start.25
  398.2 4.4 collective-permute-start.26
  404.5 7.1 collective-permute-done.26
  412.3 3.5 collective-permute-done.27
  417.2 36.8 %psum.44 = f32[256]{0:T(256)S(1)} all-reduce(f32[256]{0:T(256)S(1)} %get-tuple-element.128), channel_id=1, replica_groups=mesh['gx'=16,'gy'=2] {'gx','gy'}, use_global_device_ids=true, to_apply=%region_15.17 | all-reduce | flops 256 | bytes 2048 | tf_op jit(solution)/shard_map/psum | solution.py:61
  455.2 4.4 collective-permute-start.29
  459.6 7.0 collective-permute-done.28
  466.7 4.3 collective-permute-start.30
  478.3 24.6 %collective-permute-done.30 = f32[3,512,256]{2,1,0:T(8,128)S(1)} collective-permute-done((f32[3,512,256]{2,1,0:T(8,128)S(1)}, f32[3,512,256]{2,1,0:T(8,128)S(1)}, u32[]{:S(2)}, u32[]{:S(2)}) %collective-permute-start.30) | collective-permute-done | bytes 1572896 | tf_op jit(solution)/shard_map/ppermute | solution.py:21
  515.2 43.2 %psum.45 = f32[256]{0:T(256)S(1)} all-reduce(f32[256]{0:T(256)S(1)} %get-tuple-element.130), channel_id=1, replica_groups=mesh['gx'=16,'gy'=2] {'gx','gy'}, use_global_device_ids=true, to_apply=%region_17.19 | all-reduce | flops 256 | bytes 2048 | tf_op jit(solution)/shard_map/psum | solution.py:173
  562.8 5.2 collective-permute-done.32
  568.0 4.8 collective-permute-done.33
  574.2 4.6 collective-permute-start.35
  584.5 4.1 collective-permute-start.37
  591.4 4.4 collective-permute-start.38
  597.8 6.8 collective-permute-done.38
  609.4 36.9 %psum.46 = f32[256]{0:T(256)S(1)} all-reduce(f32[256]{0:T(256)S(1)} %get-tuple-element.132), channel_id=1, replica_groups=mesh['gx'=16,'gy'=2] {'gx','gy'}, use_global_device_ids=true, to_apply=%region_19.21 | all-reduce | flops 256 | bytes 2048 | tf_op jit(solution)/shard_map/psum | solution.py:61
  646.4 4.4 collective-permute-start.41
  650.8 7.0 collective-permute-done.40
  657.9 4.3 collective-permute-start.42
  669.3 25.0 %collective-permute-done.42 = f32[3,512,256]{2,1,0:T(8,128)S(1)} collective-permute-done((f32[3,512,256]{2,1,0:T(8,128)S(1)}, f32[3,512,256]{2,1,0:T(8,128)S(1)}, u32[]{:S(2)}, u32[]{:S(2)}) %collective-permute-start.42) | collective-permute-done | bytes 1572896 | tf_op jit(solution)/shard_map/ppermute | solution.py:21
  705.9 43.1 %psum.47 = f32[256]{0:T(256)S(1)} all-reduce(f32[256]{0:T(256)S(1)} %get-tuple-element.134), channel_id=1, replica_groups=mesh['gx'=16,'gy'=2] {'gx','gy'}, use_global_device_ids=true, to_apply=%region_21.23 | all-reduce | flops 256 | bytes 2048 | tf_op jit(solution)/shard_map/psum | solution.py:173
  (255 shorter events, 177.0 us)
Async XLA Ops:
  0.6 19.3 %copy-start = (f32[1,1,512,256]{3,2,1,0:T(8,128)S(1)}, f32[1,1,512,256]{3,2,1,0:T(8,128)}, u32[]{:S(2)}) copy-start(f32[1,1,512,256]{3,2,1,0:T(8,128)} %param.6) | copy-start | bytes 1572868
  0.7 13.4 %collective-permute-start.4 = (s32[128]{0:T(128)}, s32[128]{0:T(128)S(1)}, u32[]{:S(2)}, u32[]{:S(2)}) collective-permute-start(s32[128]{0:T(128)} %bitcast.373), channel_id=1, source_target_pairs={{0,2},{2,4},{4,6},{6,8},{8,10},{10,12},{12,14},{14,16},{16,18},{18... | collective-permute-start | bytes 1544 | tf_op jit(solution)/shard_map/ppermute | solution.py:15
  1.2 12.8 %collective-permute-start.5 = (s32[128]{0:T(128)}, s32[128]{0:T(128)S(1)}, u32[]{:S(2)}, u32[]{:S(2)}) collective-permute-start(s32[128]{0:T(128)} %bitcast.374), channel_id=1, source_target_pairs={{0,30},{2,0},{4,2},{6,4},{8,6},{10,8},{12,10},{14,12},{16,14},{18,... | collective-permute-start | bytes 1544 | tf_op jit(solution)/shard_map/ppermute | solution.py:15
  7.0 16.5 %collective-permute-start = (f32[3,512]{1,0:T(4,128)S(1)}, f32[3,512]{1,0:T(4,128)S(1)}, u32[]{:S(2)}, u32[]{:S(2)}) collective-permute-start(f32[3,512]{1,0:T(4,128)S(1)} %get-tuple-element.110), channel_id=1, source_target_pairs={{0,2},{2,4},{4,6},{6,8},{8,10},{10,12},{12,14},{14,16},{16,18},{18... | collective-permute-start | bytes 18440 | tf_op jit(solution)/shard_map/ppermute | solution.py:15
  7.0 16.4 %collective-permute-start.1 = (f32[3,512]{1,0:T(4,128)S(1)}, f32[3,512]{1,0:T(4,128)S(1)}, u32[]{:S(2)}, u32[]{:S(2)}) collective-permute-start(f32[3,512]{1,0:T(4,128)S(1)} %get-tuple-element.110), channel_id=1, source_target_pairs={{0,30},{2,0},{4,2},{6,4},{8,6},{10,8},{12,10},{14,12},{16,14},{18,... | collective-permute-start | bytes 18440 | tf_op jit(solution)/shard_map/ppermute | solution.py:15
  14.1 6.7 collective-permute-start.7
  15.4 6.3 collective-permute-start.6
  23.5 208.1 %collective-permute-start.8 = (f32[3,128,256]{2,1,0:T(8,128)}, f32[3,128,256]{2,1,0:T(8,128)}, u32[]{:S(2)}, u32[]{:S(2)}) collective-permute-start(f32[3,128,256]{2,1,0:T(8,128)} %pad_maximum_fusion.3), channel_id=1, source_target_pairs={{0,30},{2,0},{4,2},{6,4},{8,6},{10,8},{12,10},{14,12},{16,14},{18,... | collective-permute-start | bytes 1179656 | tf_op jit(solution)/shard_map/ppermute | solution.py:15
  23.5 7.5 collective-permute-start.2
  27.2 5.7 collective-permute-start.3
  29.3 202.3 %collective-permute-start.9 = (f32[3,128,256]{2,1,0:T(8,128)}, f32[3,128,256]{2,1,0:T(8,128)}, u32[]{:S(2)}, u32[]{:S(2)}) collective-permute-start(f32[3,128,256]{2,1,0:T(8,128)} %pad_maximum_fusion.4), channel_id=1, source_target_pairs={{0,2},{2,4},{4,6},{6,8},{8,10},{10,12},{12,14},{14,16},{16,18},{18... | collective-permute-start | bytes 1179656 | tf_op jit(solution)/shard_map/ppermute | solution.py:15
  170.3 54.7 %copy-start.3 = (f32[640,640]{1,0:T(8,128)S(1)}, f32[640,640]{1,0:T(8,128)}, u32[]{:S(2)}) copy-start(f32[640,640]{1,0:T(8,128)} %fusion.25) | copy-start | bytes 4915204
  232.8 11.1 %collective-permute-start.10 = (f32[128,256]{1,0:T(8,128)S(1)}, f32[128,256]{1,0:T(8,128)S(1)}, u32[]{:S(2)}, u32[]{:S(2)}) collective-permute-start(f32[128,256]{1,0:T(8,128)S(1)} %get-tuple-element.60), channel_id=1, source_target_pairs={{1,0},{3,2},{5,4},{7,6},{9,8},{11,10},{13,12},{15,14},{17,16},{19,... | collective-permute-start | bytes 393224 | tf_op jit(solution)/shard_map/ppermute | solution.py:21
  234.1 9.8 %collective-permute-start.11 = (f32[128,256]{1,0:T(8,128)S(1)}, f32[128,256]{1,0:T(8,128)S(1)}, u32[]{:S(2)}, u32[]{:S(2)}) collective-permute-start(f32[128,256]{1,0:T(8,128)S(1)} %get-tuple-element.61), channel_id=1, source_target_pairs={{0,1},{2,3},{4,5},{6,7},{8,9},{10,11},{12,13},{14,15},{16,17},{18,... | collective-permute-start | bytes 393224 | tf_op jit(solution)/shard_map/ppermute | solution.py:21
  245.7 7.1 collective-permute-start.12
  245.7 7.1 collective-permute-start.13
  252.9 6.9 collective-permute-start.14
  254.5 9.7 %collective-permute-start.15 = (f32[3,128,256]{2,1,0:T(8,128)S(1)}, f32[3,128,256]{2,1,0:T(8,128)S(1)}, u32[]{:S(2)}, u32[]{:S(2)}) collective-permute-start(f32[3,128,256]{2,1,0:T(8,128)S(1)} %pad_maximum_fusion.5), channel_id=1, source_target_pairs={{1,0},{3,2},{5,4},{7,6},{9,8},{11,10},{13,12},{15,14},{17,16},{19,... | collective-permute-start | bytes 1179656 | tf_op jit(solution)/shard_map/ppermute | solution.py:21
  264.8 11.5 %collective-permute-start.16 = (f32[512,256]{1,0:T(8,128)S(1)}, f32[512,256]{1,0:T(8,128)S(1)}, u32[]{:S(2)}, u32[]{:S(2)}) collective-permute-start(f32[512,256]{1,0:T(8,128)S(1)} %convolution_add_fusion.5), channel_id=1, source_target_pairs={{0,2},{2,4},{4,6},{6,8},{8,10},{10,12},{12,14},{14,16},{16,18},{18... | collective-permute-start | bytes 1572872 | tf_op jit(solution)/shard_map/ppermute | solution.py:15
  264.9 11.4 %collective-permute-start.17 = (f32[512,256]{1,0:T(8,128)S(1)}, f32[512,256]{1,0:T(8,128)S(1)}, u32[]{:S(2)}, u32[]{:S(2)}) collective-permute-start(f32[512,256]{1,0:T(8,128)S(1)} %convolution_add_fusion.5), channel_id=1, source_target_pairs={{0,30},{2,0},{4,2},{6,4},{8,6},{10,8},{12,10},{14,12},{16,14},{18,... | collective-permute-start | bytes 1572872 | tf_op jit(solution)/shard_map/ppermute | solution.py:15
  276.4 35.5 %collective-permute-start.18 = (f32[3,512,256]{2,1,0:T(8,128)S(1)}, f32[3,512,256]{2,1,0:T(8,128)S(1)}, u32[]{:S(2)}, u32[]{:S(2)}) collective-permute-start(f32[3,512,256]{2,1,0:T(8,128)S(1)} %pad_maximum_fusion), channel_id=1, source_target_pairs={{0,1},{2,3},{4,5},{6,7},{8,9},{10,11},{12,13},{14,15},{16,17},{18,... | collective-permute-start | bytes 4718600 | tf_op jit(solution)/shard_map/ppermute | solution.py:21
  278.0 39.5 %collective-permute-start.19 = (f32[3,512,256]{2,1,0:T(8,128)S(1)}, f32[3,512,256]{2,1,0:T(8,128)S(1)}, u32[]{:S(2)}, u32[]{:S(2)}) collective-permute-start(f32[3,512,256]{2,1,0:T(8,128)S(1)} %pad_maximum_fusion), channel_id=1, source_target_pairs={{1,0},{3,2},{5,4},{7,6},{9,8},{11,10},{13,12},{15,14},{17,16},{19,... | collective-permute-start | bytes 4718600 | tf_op jit(solution)/shard_map/ppermute | solution.py:21
  368.9 5.8 collective-permute-start.20
  369.5 10.1 %collective-permute-start.21 = (f32[3,128,256]{2,1,0:T(8,128)S(1)}, f32[3,128,256]{2,1,0:T(8,128)S(1)}, u32[]{:S(2)}, u32[]{:S(2)}) collective-permute-start(f32[3,128,256]{2,1,0:T(8,128)S(1)} %pad_maximum_fusion.7), channel_id=1, source_target_pairs={{0,2},{2,4},{4,6},{6,8},{8,10},{10,12},{12,14},{14,16},{16,18},{18... | collective-permute-start | bytes 1179656 | tf_op jit(solution)/shard_map/ppermute | solution.py:15
  379.6 7.7 %collective-permute-start.22 = (f32[128,256]{1,0:T(8,128)S(1)}, f32[128,256]{1,0:T(8,128)S(1)}, u32[]{:S(2)}, u32[]{:S(2)}) collective-permute-start(f32[128,256]{1,0:T(8,128)S(1)} %get-tuple-element.49), channel_id=1, source_target_pairs={{1,0},{3,2},{5,4},{7,6},{9,8},{11,10},{13,12},{15,14},{17,16},{19,... | collective-permute-start | bytes 393224 | tf_op jit(solution)/shard_map/ppermute | solution.py:21
  380.9 8.2 %collective-permute-start.23 = (f32[128,256]{1,0:T(8,128)S(1)}, f32[128,256]{1,0:T(8,128)S(1)}, u32[]{:S(2)}, u32[]{:S(2)}) collective-permute-start(f32[128,256]{1,0:T(8,128)S(1)} %get-tuple-element.50), channel_id=1, source_target_pairs={{0,1},{2,3},{4,5},{6,7},{8,9},{10,11},{12,13},{14,15},{16,17},{18,... | collective-permute-start | bytes 393224 | tf_op jit(solution)/shard_map/ppermute | solution.py:21
  390.9 7.2 collective-permute-start.24
  391.3 6.8 collective-permute-start.25
  398.2 13.5 %collective-permute-start.26 = (f32[3,128,256]{2,1,0:T(8,128)S(1)}, f32[3,128,256]{2,1,0:T(8,128)S(1)}, u32[]{:S(2)}, u32[]{:S(2)}) collective-permute-start(f32[3,128,256]{2,1,0:T(8,128)S(1)} %pad_maximum_fusion.8), channel_id=1, source_target_pairs={{0,1},{2,3},{4,5},{6,7},{8,9},{10,11},{12,13},{14,15},{16,17},{18,... | collective-permute-start | bytes 1179656 | tf_op jit(solution)/shard_map/ppermute | solution.py:21
  402.6 13.2 %collective-permute-start.27 = (f32[3,128,256]{2,1,0:T(8,128)S(1)}, f32[3,128,256]{2,1,0:T(8,128)S(1)}, u32[]{:S(2)}, u32[]{:S(2)}) collective-permute-start(f32[3,128,256]{2,1,0:T(8,128)S(1)} %pad_maximum_fusion.8), channel_id=1, source_target_pairs={{1,0},{3,2},{5,4},{7,6},{9,8},{11,10},{13,12},{15,14},{17,16},{19,... | collective-permute-start | bytes 1179656 | tf_op jit(solution)/shard_map/ppermute | solution.py:21
  455.1 57.2 %copy-start.1 = (f32[512,256]{1,0:T(8,128)}, f32[512,256]{1,0:T(8,128)S(1)}, u32[]{:S(2)}) copy-start(f32[512,256]{1,0:T(8,128)S(1)} %multiply_add_fusion.1) | copy-start | bytes 1572868
  455.1 11.5 %collective-permute-start.28 = (f32[512,256]{1,0:T(8,128)S(1)}, f32[512,256]{1,0:T(8,128)S(1)}, u32[]{:S(2)}, u32[]{:S(2)}) collective-permute-start(f32[512,256]{1,0:T(8,128)S(1)} %multiply_add_fusion.1), channel_id=1, source_target_pairs={{0,2},{2,4},{4,6},{6,8},{8,10},{10,12},{12,14},{14,16},{16,18},{18... | collective-permute-start | bytes 1572872 | tf_op jit(solution)/shard_map/ppermute | solution.py:15
  455.2 11.4 %collective-permute-start.29 = (f32[512,256]{1,0:T(8,128)S(1)}, f32[512,256]{1,0:T(8,128)S(1)}, u32[]{:S(2)}, u32[]{:S(2)}) collective-permute-start(f32[512,256]{1,0:T(8,128)S(1)} %multiply_add_fusion.1), channel_id=1, source_target_pairs={{0,30},{2,0},{4,2},{6,4},{8,6},{10,8},{12,10},{14,12},{16,14},{18,... | collective-permute-start | bytes 1572872 | tf_op jit(solution)/shard_map/ppermute | solution.py:15
  466.7 36.1 %collective-permute-start.30 = (f32[3,512,256]{2,1,0:T(8,128)S(1)}, f32[3,512,256]{2,1,0:T(8,128)S(1)}, u32[]{:S(2)}, u32[]{:S(2)}) collective-permute-start(f32[3,512,256]{2,1,0:T(8,128)S(1)} %pad_maximum_fusion.1), channel_id=1, source_target_pairs={{0,1},{2,3},{4,5},{6,7},{8,9},{10,11},{12,13},{14,15},{16,17},{18,... | collective-permute-start | bytes 4718600 | tf_op jit(solution)/shard_map/ppermute | solution.py:21
  471.0 37.4 %collective-permute-start.31 = (f32[3,512,256]{2,1,0:T(8,128)S(1)}, f32[3,512,256]{2,1,0:T(8,128)S(1)}, u32[]{:S(2)}, u32[]{:S(2)}) collective-permute-start(f32[3,512,256]{2,1,0:T(8,128)S(1)} %pad_maximum_fusion.1), channel_id=1, source_target_pairs={{1,0},{3,2},{5,4},{7,6},{9,8},{11,10},{13,12},{15,14},{17,16},{19,... | collective-permute-start | bytes 4718600 | tf_op jit(solution)/shard_map/ppermute | solution.py:21
  562.1 5.9 collective-permute-start.32
  562.7 10.1 %collective-permute-start.33 = (f32[3,128,256]{2,1,0:T(8,128)S(1)}, f32[3,128,256]{2,1,0:T(8,128)S(1)}, u32[]{:S(2)}, u32[]{:S(2)}) collective-permute-start(f32[3,128,256]{2,1,0:T(8,128)S(1)} %pad_maximum_fusion.10), channel_id=1, source_target_pairs={{0,2},{2,4},{4,6},{6,8},{8,10},{10,12},{12,14},{14,16},{16,18},{18... | collective-permute-start | bytes 1179656 | tf_op jit(solution)/shard_map/ppermute | solution.py:15
  572.9 7.8 %collective-permute-start.34 = (f32[128,256]{1,0:T(8,128)S(1)}, f32[128,256]{1,0:T(8,128)S(1)}, u32[]{:S(2)}, u32[]{:S(2)}) collective-permute-start(f32[128,256]{1,0:T(8,128)S(1)} %get-tuple-element.38), channel_id=1, source_target_pairs={{1,0},{3,2},{5,4},{7,6},{9,8},{11,10},{13,12},{15,14},{17,16},{19,... | collective-permute-start | bytes 393224 | tf_op jit(solution)/shard_map/ppermute | solution.py:21
  574.2 8.2 %collective-permute-start.35 = (f32[128,256]{1,0:T(8,128)S(1)}, f32[128,256]{1,0:T(8,128)S(1)}, u32[]{:S(2)}, u32[]{:S(2)}) collective-permute-start(f32[128,256]{1,0:T(8,128)S(1)} %get-tuple-element.39), channel_id=1, source_target_pairs={{0,1},{2,3},{4,5},{6,7},{8,9},{10,11},{12,13},{14,15},{16,17},{18,... | collective-permute-start | bytes 393224 | tf_op jit(solution)/shard_map/ppermute | solution.py:21
  584.2 7.2 collective-permute-start.36
  584.5 6.9 collective-permute-start.37
  591.4 13.1 %collective-permute-start.38 = (f32[3,128,256]{2,1,0:T(8,128)S(1)}, f32[3,128,256]{2,1,0:T(8,128)S(1)}, u32[]{:S(2)}, u32[]{:S(2)}) collective-permute-start(f32[3,128,256]{2,1,0:T(8,128)S(1)} %pad_maximum_fusion.11), channel_id=1, source_target_pairs={{0,1},{2,3},{4,5},{6,7},{8,9},{10,11},{12,13},{14,15},{16,17},{18,... | collective-permute-start | bytes 1179656 | tf_op jit(solution)/shard_map/ppermute | solution.py:21
  595.9 12.8 %collective-permute-start.39 = (f32[3,128,256]{2,1,0:T(8,128)S(1)}, f32[3,128,256]{2,1,0:T(8,128)S(1)}, u32[]{:S(2)}, u32[]{:S(2)}) collective-permute-start(f32[3,128,256]{2,1,0:T(8,128)S(1)} %pad_maximum_fusion.11), channel_id=1, source_target_pairs={{1,0},{3,2},{5,4},{7,6},{9,8},{11,10},{13,12},{15,14},{17,16},{19,... | collective-permute-start | bytes 1179656 | tf_op jit(solution)/shard_map/ppermute | solution.py:21
  605.2 41.1 %copy-start.2 = (f32[512,256]{1,0:T(8,128)S(1)}, f32[512,256]{1,0:T(8,128)}, u32[]{:S(2)}) copy-start(f32[512,256]{1,0:T(8,128)} %copy-done.1) | copy-start | bytes 1572868
  646.3 11.5 %collective-permute-start.40 = (f32[512,256]{1,0:T(8,128)S(1)}, f32[512,256]{1,0:T(8,128)S(1)}, u32[]{:S(2)}, u32[]{:S(2)}) collective-permute-start(f32[512,256]{1,0:T(8,128)S(1)} %multiply_add_fusion), channel_id=1, source_target_pairs={{0,2},{2,4},{4,6},{6,8},{8,10},{10,12},{12,14},{14,16},{16,18},{18... | collective-permute-start | bytes 1572872 | tf_op jit(solution)/shard_map/ppermute | solution.py:15
  646.4 11.4 %collective-permute-start.41 = (f32[512,256]{1,0:T(8,128)S(1)}, f32[512,256]{1,0:T(8,128)S(1)}, u32[]{:S(2)}, u32[]{:S(2)}) collective-permute-start(f32[512,256]{1,0:T(8,128)S(1)} %multiply_add_fusion), channel_id=1, source_target_pairs={{0,30},{2,0},{4,2},{6,4},{8,6},{10,8},{12,10},{14,12},{16,14},{18,... | collective-permute-start | bytes 1572872 | tf_op jit(solution)/shard_map/ppermute | solution.py:15
  657.9 36.3 %collective-permute-start.42 = (f32[3,512,256]{2,1,0:T(8,128)S(1)}, f32[3,512,256]{2,1,0:T(8,128)S(1)}, u32[]{:S(2)}, u32[]{:S(2)}) collective-permute-start(f32[3,512,256]{2,1,0:T(8,128)S(1)} %pad_maximum_fusion.2), channel_id=1, source_target_pairs={{0,1},{2,3},{4,5},{6,7},{8,9},{10,11},{12,13},{14,15},{16,17},{18,... | collective-permute-start | bytes 4718600 | tf_op jit(solution)/shard_map/ppermute | solution.py:21
  662.2 37.6 %collective-permute-start.43 = (f32[3,512,256]{2,1,0:T(8,128)S(1)}, f32[3,512,256]{2,1,0:T(8,128)S(1)}, u32[]{:S(2)}, u32[]{:S(2)}) collective-permute-start(f32[3,512,256]{2,1,0:T(8,128)S(1)} %pad_maximum_fusion.2), channel_id=1, source_target_pairs={{1,0},{3,2},{5,4},{7,6},{9,8},{11,10},{13,12},{15,14},{17,16},{19,... | collective-permute-start | bytes 4718600 | tf_op jit(solution)/shard_map/ppermute | solution.py:21
  (5 other events, 28.6 us)
where the time goes:
time: 756 us; the launch traced here: 751 us
  blocking collectives  201 us (27%)
  other arithmetic  168 us (22%)
  waiting for transfers between devices  161 us (21%)
  starting transfers between devices  96.9 us (13%)
  matrix products  94.8 us (13%)
  local copies, waits for them, and re-layouts  22.5 us (3%)
    psum x3, blocking collectives, residual_dot(): return lax.psum(column_sum(residue, precond), ('gx', 'gy'))  115 us
    ppermute x22, waiting for transfers between devices, passed_along(): return lax.ppermute(block, axis, route)  112 us
    another operation x19, other arithmetic, shards(): factor = jnp.linalg.cholesky(local_matrix)  101 us
    psum x2, blocking collectives, shards(): lax.psum(column_sum(direction, accumulated), ('gx', 'gy'))  86.3 us
    ppermute x22, starting transfers between devices, passed_along(): return lax.ppermute(block, axis, route)  57.9 us
    dot_general x27, matrix products, shards(): jnp.dot(kernel_block(own_pos, positions[operate_row_off][operate_col_off]...  52.9 us
    another operation x3, other arithmetic, shards(): lax.linalg.triangular_solve(factor, jnp.eye(ext_len, dtype=jnp.float32),...  52 us
    ppermute x22, waiting for transfers between devices, shifted(): lax.ppermute(value, axis, [(i, (i + by) % count) for i in range(count)])  49 us
  transfers between devices with their start and end apart: 44, of which 24 were waited for; matrix products, arithmetic and copies ran while one was open for 33% of the time, Pallas kernels for 0%

commit v1 on v0

--- a/solution.py
+++ b/solution.py
@@ -170,7 +170,7 @@
                     precision=HIGH,
                     preferred_element_type=jnp.float32,
                 )
-        step_size = inner_now / lax.psum(column_sum(direction, accumulated), ("gx", "gy"))
+        step_size = inner_now / lax.psum(lax.psum(column_sum(direction, accumulated), "gx"), "gy")
         solution = solution + step_size * direction
         residual = residual - step_size * accumulated
         if iteration + 1 < ITERS:

time: 756 us -> 780 us (1.032)
  blocking collectives: 201 us -> 232 us
  waiting for transfers between devices: 161 us -> 152 us
    psum x2 -> x6, blocking collectives: 86.3 us -> 119 us  [the longest x3 103 us: shards(): lax.psum(column_sum(direction, accumulated), 'gx')]
    ppermute x22, waiting for transfers between devices: 112 us -> 104 us  [passed_along(): return lax.ppermute(block, axis, route)]
  transfers between devices with their start and end apart: 44 -> 44, of which waited for: 24 -> 24; matrix products, arithmetic and copies ran while one was open for 33% -> 32% of each run, Pallas kernels for 0% -> 0%
where the time goes in v1:
time: 780 us; the launch traced here: 775 us
  blocking collectives  232 us (30%)
  other arithmetic  168 us (22%)
  waiting for transfers between devices  152 us (19%)
  starting transfers between devices  99.4 us (13%)
  matrix products  94.8 us (12%)
  local copies, waits for them, and re-layouts  22.7 us (3%)
    psum x3, blocking collectives, residual_dot(): return lax.psum(column_sum(residue, precond), ('gx', 'gy'))  114 us
    ppermute x22, waiting for transfers between devices, passed_along(): return lax.ppermute(block, axis, route)  104 us
    psum x3, blocking collectives, shards(): lax.psum(column_sum(direction, accumulated), 'gx')  103 us
    another operation x19, other arithmetic, shards(): factor = jnp.linalg.cholesky(local_matrix)  101 us
    ppermute x22, starting transfers between devices, passed_along(): return lax.ppermute(block, axis, route)  57.8 us
    dot_general x27, matrix products, shards(): jnp.dot(kernel_block(own_pos, positions[operate_row_off][operate_col_off]...  52.9 us
    another operation x3, other arithmetic, shards(): lax.linalg.triangular_solve(factor, jnp.eye(ext_len, dtype=jnp.float32),...  52 us
    ppermute x22, waiting for transfers between devices, shifted(): lax.ppermute(value, axis, [(i, (i + by) % count) for i in range(count)])  48.1 us
  transfers between devices with their start and end apart: 44, of which 24 were waited for; matrix products, arithmetic and copies ran while one was open for 32% of the time, Pallas kernels for 0%

profile of v1, /device:TPU:0, one launch (start us, length us, event | category | flops | bytes accessed | tf_op | source)
XLA Modules:
  0.0 775.2 jit_solution(3295732440265664145)
XLA Ops:
  1.2 5.0 collective-permute-start.5
  7.0 4.4 collective-permute-start.1
  15.4 4.5 collective-permute-start.6
  38.7 11.7 %cholesky.132 = f32[128,128]{1,0:T(8,128)S(1)} custom-call(f32[128,128]{1,0:T(8,128)S(1)} %cholesky.337), custom_call_target="Cholesky" | custom-call | tf_op jit(solution)/shard_map/jit(cholesky)/cholesky | solution.py:108
  50.5 9.8 %custom-call.38 = f32[1,128,128]{1,2,0:T(8,128)S(1)} custom-call(f32[1,128,128]{2,1,0:T(8,128)S(1)} %get-tuple-element.81), custom_call_target="InvertDiagBlocksLowerTriangular" | custom-call | tf_op jit(solution)/shard_map/jit(cholesky)/cholesky | solution.py:108
  63.0 11.9 %cholesky.270 = f32[128,128]{1,0:T(8,128)S(1)} custom-call(f32[128,128]{1,0:T(8,128)S(1)} %cholesky.341), custom_call_target="Cholesky" | custom-call | tf_op jit(solution)/shard_map/jit(cholesky)/cholesky | solution.py:108
  76.3 9.8 %custom-call.39 = f32[1,128,128]{1,2,0:T(8,128)S(1)} custom-call(f32[1,128,128]{2,1,0:T(8,128)S(1)} %get-tuple-element.78), custom_call_target="InvertDiagBlocksLowerTriangular" | custom-call | tf_op jit(solution)/shard_map/jit(cholesky)/cholesky | solution.py:108
  87.8 11.7 %cholesky.291 = f32[128,128]{1,0:T(8,128)S(1)} custom-call(f32[128,128]{1,0:T(8,128)S(1)} %cholesky.346), custom_call_target="Cholesky" | custom-call | tf_op jit(solution)/shard_map/jit(cholesky)/cholesky | solution.py:108
  100.2 9.8 %custom-call.40 = f32[1,128,128]{1,2,0:T(8,128)S(1)} custom-call(f32[1,128,128]{2,1,0:T(8,128)S(1)} %get-tuple-element.75), custom_call_target="InvertDiagBlocksLowerTriangular" | custom-call | tf_op jit(solution)/shard_map/jit(cholesky)/cholesky | solution.py:108
  111.9 11.7 %cholesky.310 = f32[128,128]{1,0:T(8,128)S(1)} custom-call(f32[128,128]{1,0:T(8,128)S(1)} %cholesky.351), custom_call_target="Cholesky" | custom-call | tf_op jit(solution)/shard_map/jit(cholesky)/cholesky | solution.py:108
  124.3 9.8 %custom-call.41 = f32[1,128,128]{1,2,0:T(8,128)S(1)} custom-call(f32[1,128,128]{2,1,0:T(8,128)S(1)} %get-tuple-element.72), custom_call_target="InvertDiagBlocksLowerTriangular" | custom-call | tf_op jit(solution)/shard_map/jit(cholesky)/cholesky | solution.py:108
  135.6 11.7 %cholesky.327 = f32[128,128]{1,0:T(8,128)S(1)} custom-call(f32[128,128]{1,0:T(8,128)S(1)} %convolution_subtract_fusion.6), custom_call_target="Cholesky" | custom-call | tf_op jit(solution)/shard_map/jit(cholesky)/cholesky | solution.py:108
  152.2 18.0 %while.1 = (s32[]{:T(128)}, f32[640,640]{1,0:T(8,128)}, s32[5,2]{0,1:T(2,128)S(1)}, f32[5,128,128]{2,1,0:T(8,128)}, s32[]{:T(128)}) while((s32[]{:T(128)}, f32[640,640]{1,0:T(8,128)}, s32[5,2]{0,1:T(2,128)S(1)}, f32[5,128,128]{2,1,0:T(8,128)}, s32[]{:T(128)}) %tuple.96), condition=%wide.while_cond, body=%wide.while_body.sunk | while | flops 2 | bytes 132705 | solution.py:109
  170.2 50.7 %custom-call.42 = f32[5,128,128]{1,2,0:T(8,128)} custom-call(f32[5,128,128]{2,1,0:T(8,128)} %get-tuple-element.10), custom_call_target="InvertDiagBlocksLowerTriangular" | custom-call | tf_op jit(solution)/shard_map/triangular_solve | solution.py:109
  234.0 4.7 collective-permute-start.11
  238.7 5.0 fusion.240
  245.6 4.4 collective-permute-start.13
  264.7 4.4 collective-permute-start.17
  269.2 6.9 collective-permute-done.16
  285.2 26.6 %collective-permute-done.18 = f32[3,512,256]{2,1,0:T(8,128)S(1)} collective-permute-done((f32[3,512,256]{2,1,0:T(8,128)S(1)}, f32[3,512,256]{2,1,0:T(8,128)S(1)}, u32[]{:S(2)}, u32[]{:S(2)}) %collective-permute-start.18) | collective-permute-done | bytes 1572896 | tf_op jit(solution)/shard_map/ppermute | solution.py:21
  324.1 32.9 %psum.64 = f32[256]{0:T(256)S(1)} all-reduce(f32[256]{0:T(256)S(1)} %get-tuple-element.11), channel_id=1, replica_groups=mesh['gx'=16,'gy'=2] {'gx'}, use_global_device_ids=true, to_apply=%region_13.15 | all-reduce | flops 256 | bytes 2048 | tf_op jit(solution)/shard_map/psum | solution.py:173
  357.1 5.4 psum.65
  362.4 36.9 %psum.63 = f32[256]{0:T(256)S(1)} all-reduce(f32[256]{0:T(256)S(1)} %get-tuple-element.12), channel_id=1, replica_groups=mesh['gx'=16,'gy'=2] {'gx','gy'}, use_global_device_ids=true, to_apply=%region_11.13 | all-reduce | flops 256 | bytes 2048 | tf_op jit(solution)/shard_map/psum | solution.py:61
  406.3 5.2 collective-permute-done.20
  411.5 4.7 collective-permute-done.21
  417.6 4.6 collective-permute-start.23
  426.5 4.4 collective-permute-start.25
  433.6 4.4 collective-permute-start.26
  439.9 4.7 collective-permute-done.26
  450.1 39.4 %psum.66 = f32[256]{0:T(256)S(1)} all-reduce(f32[256]{0:T(256)S(1)} %get-tuple-element.126), channel_id=1, replica_groups=mesh['gx'=16,'gy'=2] {'gx','gy'}, use_global_device_ids=true, to_apply=%region_16.18 | all-reduce | flops 256 | bytes 2048 | tf_op jit(solution)/shard_map/psum | solution.py:61
  490.7 4.4 collective-permute-start.29
  495.2 7.0 collective-permute-done.28
  502.3 4.3 collective-permute-start.30
  513.8 23.5 %collective-permute-done.30 = f32[3,512,256]{2,1,0:T(8,128)S(1)} collective-permute-done((f32[3,512,256]{2,1,0:T(8,128)S(1)}, f32[3,512,256]{2,1,0:T(8,128)S(1)}, u32[]{:S(2)}, u32[]{:S(2)}) %collective-permute-start.30) | collective-permute-done | bytes 1572896 | tf_op jit(solution)/shard_map/ppermute | solution.py:21
  549.7 35.1 %psum.67 = f32[256]{0:T(256)S(1)} all-reduce(f32[256]{0:T(256)S(1)} %get-tuple-element.128), channel_id=1, replica_groups=mesh['gx'=16,'gy'=2] {'gx'}, use_global_device_ids=true, to_apply=%region_18.20 | all-reduce | flops 256 | bytes 2048 | tf_op jit(solution)/shard_map/psum | solution.py:173
  584.7 5.4 psum.68
  594.5 4.7 collective-permute-done.32
  599.2 4.7 collective-permute-done.33
  605.3 4.6 collective-permute-start.35
  614.2 4.4 collective-permute-start.37
  621.3 4.4 collective-permute-start.38
  636.0 37.2 %psum.69 = f32[256]{0:T(256)S(1)} all-reduce(f32[256]{0:T(256)S(1)} %get-tuple-element.130), channel_id=1, replica_groups=mesh['gx'=16,'gy'=2] {'gx','gy'}, use_global_device_ids=true, to_apply=%region_21.23 | all-reduce | flops 256 | bytes 2048 | tf_op jit(solution)/shard_map/psum | solution.py:61
  673.4 4.4 collective-permute-start.41
  677.9 7.0 collective-permute-done.40
  684.9 4.3 collective-permute-start.42
  696.3 25.6 %collective-permute-done.42 = f32[3,512,256]{2,1,0:T(8,128)S(1)} collective-permute-done((f32[3,512,256]{2,1,0:T(8,128)S(1)}, f32[3,512,256]{2,1,0:T(8,128)S(1)}, u32[]{:S(2)}, u32[]{:S(2)}) %collective-permute-start.42) | collective-permute-done | bytes 1572896 | tf_op jit(solution)/shard_map/ppermute | solution.py:21
  733.5 34.7 %psum.70 = f32[256]{0:T(256)S(1)} all-reduce(f32[256]{0:T(256)S(1)} %get-tuple-element.132), channel_id=1, replica_groups=mesh['gx'=16,'gy'=2] {'gx'}, use_global_device_ids=true, to_apply=%region_23.25 | all-reduce | flops 256 | bytes 2048 | tf_op jit(solution)/shard_map/psum | solution.py:173
  768.2 5.4 psum.71
  (259 shorter events, 191.2 us)
Async XLA Ops:
  0.6 19.3 %copy-start = (f32[1,1,512,256]{3,2,1,0:T(8,128)S(1)}, f32[1,1,512,256]{3,2,1,0:T(8,128)}, u32[]{:S(2)}) copy-start(f32[1,1,512,256]{3,2,1,0:T(8,128)} %param.6) | copy-start | bytes 1572868
  0.7 13.4 %collective-permute-start.4 = (s32[128]{0:T(128)}, s32[128]{0:T(128)S(1)}, u32[]{:S(2)}, u32[]{:S(2)}) collective-permute-start(s32[128]{0:T(128)} %bitcast.373), channel_id=1, source_target_pairs={{0,2},{2,4},{4,6},{6,8},{8,10},{10,12},{12,14},{14,16},{16,18},{18... | collective-permute-start | bytes 1544 | tf_op jit(solution)/shard_map/ppermute | solution.py:15
  1.2 12.8 %collective-permute-start.5 = (s32[128]{0:T(128)}, s32[128]{0:T(128)S(1)}, u32[]{:S(2)}, u32[]{:S(2)}) collective-permute-start(s32[128]{0:T(128)} %bitcast.374), channel_id=1, source_target_pairs={{0,30},{2,0},{4,2},{6,4},{8,6},{10,8},{12,10},{14,12},{16,14},{18,... | collective-permute-start | bytes 1544 | tf_op jit(solution)/shard_map/ppermute | solution.py:15
  7.0 16.5 %collective-permute-start = (f32[3,512]{1,0:T(4,128)S(1)}, f32[3,512]{1,0:T(4,128)S(1)}, u32[]{:S(2)}, u32[]{:S(2)}) collective-permute-start(f32[3,512]{1,0:T(4,128)S(1)} %get-tuple-element.108), channel_id=1, source_target_pairs={{0,2},{2,4},{4,6},{6,8},{8,10},{10,12},{12,14},{14,16},{16,18},{18... | collective-permute-start | bytes 18440 | tf_op jit(solution)/shard_map/ppermute | solution.py:15
  7.0 16.4 %collective-permute-start.1 = (f32[3,512]{1,0:T(4,128)S(1)}, f32[3,512]{1,0:T(4,128)S(1)}, u32[]{:S(2)}, u32[]{:S(2)}) collective-permute-start(f32[3,512]{1,0:T(4,128)S(1)} %get-tuple-element.108), channel_id=1, source_target_pairs={{0,30},{2,0},{4,2},{6,4},{8,6},{10,8},{12,10},{14,12},{16,14},{18,... | collective-permute-start | bytes 18440 | tf_op jit(solution)/shard_map/ppermute | solution.py:15
  14.1 6.7 collective-permute-start.7
  15.4 6.3 collective-permute-start.6
  23.4 208.0 %collective-permute-start.8 = (f32[3,128,256]{2,1,0:T(8,128)}, f32[3,128,256]{2,1,0:T(8,128)}, u32[]{:S(2)}, u32[]{:S(2)}) collective-permute-start(f32[3,128,256]{2,1,0:T(8,128)} %pad_maximum_fusion.3), channel_id=1, source_target_pairs={{0,30},{2,0},{4,2},{6,4},{8,6},{10,8},{12,10},{14,12},{16,14},{18,... | collective-permute-start | bytes 1179656 | tf_op jit(solution)/shard_map/ppermute | solution.py:15
  23.5 7.5 collective-permute-start.2
  27.2 5.7 collective-permute-start.3
  29.3 202.2 %collective-permute-start.9 = (f32[3,128,256]{2,1,0:T(8,128)}, f32[3,128,256]{2,1,0:T(8,128)}, u32[]{:S(2)}, u32[]{:S(2)}) collective-permute-start(f32[3,128,256]{2,1,0:T(8,128)} %pad_maximum_fusion.4), channel_id=1, source_target_pairs={{0,2},{2,4},{4,6},{6,8},{8,10},{10,12},{12,14},{14,16},{16,18},{18... | collective-permute-start | bytes 1179656 | tf_op jit(solution)/shard_map/ppermute | solution.py:15
  170.2 54.7 %copy-start.3 = (f32[640,640]{1,0:T(8,128)S(1)}, f32[640,640]{1,0:T(8,128)}, u32[]{:S(2)}) copy-start(f32[640,640]{1,0:T(8,128)} %fusion.25) | copy-start | bytes 4915204
  232.7 11.1 %collective-permute-start.10 = (f32[128,256]{1,0:T(8,128)S(1)}, f32[128,256]{1,0:T(8,128)S(1)}, u32[]{:S(2)}, u32[]{:S(2)}) collective-permute-start(f32[128,256]{1,0:T(8,128)S(1)} %get-tuple-element.58), channel_id=1, source_target_pairs={{1,0},{3,2},{5,4},{7,6},{9,8},{11,10},{13,12},{15,14},{17,16},{19,... | collective-permute-start | bytes 393224 | tf_op jit(solution)/shard_map/ppermute | solution.py:21
  234.0 9.8 %collective-permute-start.11 = (f32[128,256]{1,0:T(8,128)S(1)}, f32[128,256]{1,0:T(8,128)S(1)}, u32[]{:S(2)}, u32[]{:S(2)}) collective-permute-start(f32[128,256]{1,0:T(8,128)S(1)} %get-tuple-element.59), channel_id=1, source_target_pairs={{0,1},{2,3},{4,5},{6,7},{8,9},{10,11},{12,13},{14,15},{16,17},{18,... | collective-permute-start | bytes 393224 | tf_op jit(solution)/shard_map/ppermute | solution.py:21
  245.6 7.1 collective-permute-start.12
  245.6 7.1 collective-permute-start.13
  252.7 6.9 collective-permute-start.14
  254.4 9.7 %collective-permute-start.15 = (f32[3,128,256]{2,1,0:T(8,128)S(1)}, f32[3,128,256]{2,1,0:T(8,128)S(1)}, u32[]{:S(2)}, u32[]{:S(2)}) collective-permute-start(f32[3,128,256]{2,1,0:T(8,128)S(1)} %pad_maximum_fusion.5), channel_id=1, source_target_pairs={{1,0},{3,2},{5,4},{7,6},{9,8},{11,10},{13,12},{15,14},{17,16},{19,... | collective-permute-start | bytes 1179656 | tf_op jit(solution)/shard_map/ppermute | solution.py:21
  264.7 11.5 %collective-permute-start.16 = (f32[512,256]{1,0:T(8,128)S(1)}, f32[512,256]{1,0:T(8,128)S(1)}, u32[]{:S(2)}, u32[]{:S(2)}) collective-permute-start(f32[512,256]{1,0:T(8,128)S(1)} %convolution_add_fusion.5), channel_id=1, source_target_pairs={{0,2},{2,4},{4,6},{6,8},{8,10},{10,12},{12,14},{14,16},{16,18},{18... | collective-permute-start | bytes 1572872 | tf_op jit(solution)/shard_map/ppermute | solution.py:15
  264.7 11.4 %collective-permute-start.17 = (f32[512,256]{1,0:T(8,128)S(1)}, f32[512,256]{1,0:T(8,128)S(1)}, u32[]{:S(2)}, u32[]{:S(2)}) collective-permute-start(f32[512,256]{1,0:T(8,128)S(1)} %convolution_add_fusion.5), channel_id=1, source_target_pairs={{0,30},{2,0},{4,2},{6,4},{8,6},{10,8},{12,10},{14,12},{16,14},{18,... | collective-permute-start | bytes 1572872 | tf_op jit(solution)/shard_map/ppermute | solution.py:15
  276.3 35.5 %collective-permute-start.18 = (f32[3,512,256]{2,1,0:T(8,128)S(1)}, f32[3,512,256]{2,1,0:T(8,128)S(1)}, u32[]{:S(2)}, u32[]{:S(2)}) collective-permute-start(f32[3,512,256]{2,1,0:T(8,128)S(1)} %pad_maximum_fusion), channel_id=1, source_target_pairs={{0,1},{2,3},{4,5},{6,7},{8,9},{10,11},{12,13},{14,15},{16,17},{18,... | collective-permute-start | bytes 4718600 | tf_op jit(solution)/shard_map/ppermute | solution.py:21
  277.9 39.5 %collective-permute-start.19 = (f32[3,512,256]{2,1,0:T(8,128)S(1)}, f32[3,512,256]{2,1,0:T(8,128)S(1)}, u32[]{:S(2)}, u32[]{:S(2)}) collective-permute-start(f32[3,512,256]{2,1,0:T(8,128)S(1)} %pad_maximum_fusion), channel_id=1, source_target_pairs={{1,0},{3,2},{5,4},{7,6},{9,8},{11,10},{13,12},{15,14},{17,16},{19,... | collective-permute-start | bytes 4718600 | tf_op jit(solution)/shard_map/ppermute | solution.py:21
  403.0 8.5 %collective-permute-start.20 = (f32[3,128,256]{2,1,0:T(8,128)S(1)}, f32[3,128,256]{2,1,0:T(8,128)S(1)}, u32[]{:S(2)}, u32[]{:S(2)}) collective-permute-start(f32[3,128,256]{2,1,0:T(8,128)S(1)} %pad_maximum_fusion.6), channel_id=1, source_target_pairs={{0,30},{2,0},{4,2},{6,4},{8,6},{10,8},{12,10},{14,12},{16,14},{18,... | collective-permute-start | bytes 1179656 | tf_op jit(solution)/shard_map/ppermute | solution.py:15
  406.2 10.0 %collective-permute-start.21 = (f32[3,128,256]{2,1,0:T(8,128)S(1)}, f32[3,128,256]{2,1,0:T(8,128)S(1)}, u32[]{:S(2)}, u32[]{:S(2)}) collective-permute-start(f32[3,128,256]{2,1,0:T(8,128)S(1)} %pad_maximum_fusion.7), channel_id=1, source_target_pairs={{0,2},{2,4},{4,6},{6,8},{8,10},{10,12},{12,14},{14,16},{16,18},{18... | collective-permute-start | bytes 1179656 | tf_op jit(solution)/shard_map/ppermute | solution.py:15
  416.3 6.9 collective-permute-start.22
  417.6 7.1 collective-permute-start.23
  426.4 7.1 collective-permute-start.24
  426.5 7.1 collective-permute-start.25
  433.6 11.0 %collective-permute-start.26 = (f32[3,128,256]{2,1,0:T(8,128)S(1)}, f32[3,128,256]{2,1,0:T(8,128)S(1)}, u32[]{:S(2)}, u32[]{:S(2)}) collective-permute-start(f32[3,128,256]{2,1,0:T(8,128)S(1)} %pad_maximum_fusion.8), channel_id=1, source_target_pairs={{0,1},{2,3},{4,5},{6,7},{8,9},{10,11},{12,13},{14,15},{16,17},{18,... | collective-permute-start | bytes 1179656 | tf_op jit(solution)/shard_map/ppermute | solution.py:21
  437.9 10.7 %collective-permute-start.27 = (f32[3,128,256]{2,1,0:T(8,128)S(1)}, f32[3,128,256]{2,1,0:T(8,128)S(1)}, u32[]{:S(2)}, u32[]{:S(2)}) collective-permute-start(f32[3,128,256]{2,1,0:T(8,128)S(1)} %pad_maximum_fusion.8), channel_id=1, source_target_pairs={{1,0},{3,2},{5,4},{7,6},{9,8},{11,10},{13,12},{15,14},{17,16},{19,... | collective-permute-start | bytes 1179656 | tf_op jit(solution)/shard_map/ppermute | solution.py:21
  490.7 56.2 %copy-start.1 = (f32[512,256]{1,0:T(8,128)}, f32[512,256]{1,0:T(8,128)S(1)}, u32[]{:S(2)}) copy-start(f32[512,256]{1,0:T(8,128)S(1)} %multiply_add_fusion.1) | copy-start | bytes 1572868
  490.7 11.5 %collective-permute-start.28 = (f32[512,256]{1,0:T(8,128)S(1)}, f32[512,256]{1,0:T(8,128)S(1)}, u32[]{:S(2)}, u32[]{:S(2)}) collective-permute-start(f32[512,256]{1,0:T(8,128)S(1)} %multiply_add_fusion.1), channel_id=1, source_target_pairs={{0,2},{2,4},{4,6},{6,8},{8,10},{10,12},{12,14},{14,16},{16,18},{18... | collective-permute-start | bytes 1572872 | tf_op jit(solution)/shard_map/ppermute | solution.py:15
  490.7 11.4 %collective-permute-start.29 = (f32[512,256]{1,0:T(8,128)S(1)}, f32[512,256]{1,0:T(8,128)S(1)}, u32[]{:S(2)}, u32[]{:S(2)}) collective-permute-start(f32[512,256]{1,0:T(8,128)S(1)} %multiply_add_fusion.1), channel_id=1, source_target_pairs={{0,30},{2,0},{4,2},{6,4},{8,6},{10,8},{12,10},{14,12},{16,14},{18,... | collective-permute-start | bytes 1572872 | tf_op jit(solution)/shard_map/ppermute | solution.py:15
  502.3 35.1 %collective-permute-start.30 = (f32[3,512,256]{2,1,0:T(8,128)S(1)}, f32[3,512,256]{2,1,0:T(8,128)S(1)}, u32[]{:S(2)}, u32[]{:S(2)}) collective-permute-start(f32[3,512,256]{2,1,0:T(8,128)S(1)} %pad_maximum_fusion.1), channel_id=1, source_target_pairs={{0,1},{2,3},{4,5},{6,7},{8,9},{10,11},{12,13},{14,15},{16,17},{18,... | collective-permute-start | bytes 4718600 | tf_op jit(solution)/shard_map/ppermute | solution.py:21
  506.5 36.4 %collective-permute-start.31 = (f32[3,512,256]{2,1,0:T(8,128)S(1)}, f32[3,512,256]{2,1,0:T(8,128)S(1)}, u32[]{:S(2)}, u32[]{:S(2)}) collective-permute-start(f32[3,512,256]{2,1,0:T(8,128)S(1)} %pad_maximum_fusion.1), channel_id=1, source_target_pairs={{1,0},{3,2},{5,4},{7,6},{9,8},{11,10},{13,12},{15,14},{17,16},{19,... | collective-permute-start | bytes 4718600 | tf_op jit(solution)/shard_map/ppermute | solution.py:21
  593.8 5.4 collective-permute-start.32
  593.9 10.0 %collective-permute-start.33 = (f32[3,128,256]{2,1,0:T(8,128)S(1)}, f32[3,128,256]{2,1,0:T(8,128)S(1)}, u32[]{:S(2)}, u32[]{:S(2)}) collective-permute-start(f32[3,128,256]{2,1,0:T(8,128)S(1)} %pad_maximum_fusion.10), channel_id=1, source_target_pairs={{0,2},{2,4},{4,6},{6,8},{8,10},{10,12},{12,14},{14,16},{16,18},{18... | collective-permute-start | bytes 1179656 | tf_op jit(solution)/shard_map/ppermute | solution.py:15
  604.0 6.9 collective-permute-start.34
  605.3 7.1 collective-permute-start.35
  614.1 7.1 collective-permute-start.36
  614.2 7.1 collective-permute-start.37
  621.3 9.6 %collective-permute-start.38 = (f32[3,128,256]{2,1,0:T(8,128)S(1)}, f32[3,128,256]{2,1,0:T(8,128)S(1)}, u32[]{:S(2)}, u32[]{:S(2)}) collective-permute-start(f32[3,128,256]{2,1,0:T(8,128)S(1)} %pad_maximum_fusion.11), channel_id=1, source_target_pairs={{0,1},{2,3},{4,5},{6,7},{8,9},{10,11},{12,13},{14,15},{16,17},{18,... | collective-permute-start | bytes 1179656 | tf_op jit(solution)/shard_map/ppermute | solution.py:21
  625.7 9.7 %collective-permute-start.39 = (f32[3,128,256]{2,1,0:T(8,128)S(1)}, f32[3,128,256]{2,1,0:T(8,128)S(1)}, u32[]{:S(2)}, u32[]{:S(2)}) collective-permute-start(f32[3,128,256]{2,1,0:T(8,128)S(1)} %pad_maximum_fusion.11), channel_id=1, source_target_pairs={{1,0},{3,2},{5,4},{7,6},{9,8},{11,10},{13,12},{15,14},{17,16},{19,... | collective-permute-start | bytes 1179656 | tf_op jit(solution)/shard_map/ppermute | solution.py:21
  631.5 41.8 %copy-start.2 = (f32[512,256]{1,0:T(8,128)S(1)}, f32[512,256]{1,0:T(8,128)}, u32[]{:S(2)}) copy-start(f32[512,256]{1,0:T(8,128)} %copy-done.1) | copy-start | bytes 1572868
  673.4 11.5 %collective-permute-start.40 = (f32[512,256]{1,0:T(8,128)S(1)}, f32[512,256]{1,0:T(8,128)S(1)}, u32[]{:S(2)}, u32[]{:S(2)}) collective-permute-start(f32[512,256]{1,0:T(8,128)S(1)} %multiply_add_fusion), channel_id=1, source_target_pairs={{0,2},{2,4},{4,6},{6,8},{8,10},{10,12},{12,14},{14,16},{16,18},{18... | collective-permute-start | bytes 1572872 | tf_op jit(solution)/shard_map/ppermute | solution.py:15
  673.4 11.4 %collective-permute-start.41 = (f32[512,256]{1,0:T(8,128)S(1)}, f32[512,256]{1,0:T(8,128)S(1)}, u32[]{:S(2)}, u32[]{:S(2)}) collective-permute-start(f32[512,256]{1,0:T(8,128)S(1)} %multiply_add_fusion), channel_id=1, source_target_pairs={{0,30},{2,0},{4,2},{6,4},{8,6},{10,8},{12,10},{14,12},{16,14},{18,... | collective-permute-start | bytes 1572872 | tf_op jit(solution)/shard_map/ppermute | solution.py:15
  684.9 37.0 %collective-permute-start.42 = (f32[3,512,256]{2,1,0:T(8,128)S(1)}, f32[3,512,256]{2,1,0:T(8,128)S(1)}, u32[]{:S(2)}, u32[]{:S(2)}) collective-permute-start(f32[3,512,256]{2,1,0:T(8,128)S(1)} %pad_maximum_fusion.2), channel_id=1, source_target_pairs={{0,1},{2,3},{4,5},{6,7},{8,9},{10,11},{12,13},{14,15},{16,17},{18,... | collective-permute-start | bytes 4718600 | tf_op jit(solution)/shard_map/ppermute | solution.py:21
  689.2 38.3 %collective-permute-start.43 = (f32[3,512,256]{2,1,0:T(8,128)S(1)}, f32[3,512,256]{2,1,0:T(8,128)S(1)}, u32[]{:S(2)}, u32[]{:S(2)}) collective-permute-start(f32[3,512,256]{2,1,0:T(8,128)S(1)} %pad_maximum_fusion.2), channel_id=1, source_target_pairs={{1,0},{3,2},{5,4},{7,6},{9,8},{11,10},{13,12},{15,14},{17,16},{19,... | collective-permute-start | bytes 4718600 | tf_op jit(solution)/shard_map/ppermute | solution.py:21
  (5 other events, 28.5 us)
